TPU v7x, 256 devices: a whole 4x4x8 slice. The times are simulated.
256 devices in a mesh: row: 32 (over z, y), feat: 8 (over x, core).
Axes of the slice: x: 4, y: 4, z: 8, core: 2. Of those that a mesh axis runs over, the one named last changes fastest.
Arguments:
- design: bfloat16 [4096, 65536], P('row', 'feat'), may hold values from -0.0234375 to 0.0234375
- targets: bfloat16 [4096, 48], P('row'), may hold values from -6 to 6
- factor: float32 [65536, 256], P(('feat', 'row')), may hold values from -0.09375 to 0.09375
- weights: float32 [256], replicated, may hold values from 0.3 to 3
- penalty: float32 [48], replicated, may hold values from 0.05 to 0.5
Outputs:
- solution: float32 [65536, 48], P(('feat', 'row'))
- residual: float32 [65536, 48], P(('feat', 'row'))
All inputs are finite; a program needn't handle non-finite values.
Results may differ from a plain program's by a relative error of at most 0.024.
Values may be sent and summed in bfloat16 or wider, within the bound.
No kernel may reach another device: no remote copies, remote signals or barrier semaphores. Data moves between devices by JAX's collectives and lax.ppermute only.
A program may use at most 64 MiB of HBM per device.

v0:
```python
import jax
import jax.numpy as jnp
from jax import lax
from jax.sharding import Mesh
from jax.sharding import PartitionSpec as P

ITERS = 3
ROW = ("row_0", "row_1")
ROW_FEAT = ("row_0", "row_1", "feat_0", "feat_1")
FEAT = ("feat_0", "feat_1")
FEAT_ROW = ("feat_0", "feat_1", "row_0", "row_1")


def in_blocks(shard, dim, devices):
    lengths = shard.shape
    pieces = shard.reshape(*lengths[:dim], devices, lengths[dim] // devices, *lengths[dim + 1 :])
    return jnp.moveaxis(pieces, dim, 0)


def summed_on_arrival(shard, axis, dim):
    pieces = in_blocks(shard, dim, lax.axis_size(axis))
    arrived = lax.all_to_all(pieces, axis, split_axis=0, concat_axis=0, tiled=True)
    return arrived.sum(axis=0)


def joined_along(pieces, dim):
    lengths = list(pieces.shape[1:])
    lengths[dim] *= pieces.shape[0]
    return jnp.moveaxis(pieces, 0, dim).reshape(lengths)


def copy_for_each(shard, axis):
    devices = lax.axis_size(axis)
    return lax.all_to_all(
        jnp.broadcast_to(shard[None], (devices, *shard.shape)), axis, 0, 0, tiled=True
    )


def collect(shard, axis, dim):
    return joined_along(copy_for_each(shard, axis), dim)


def one_axis_at_a_time(shard, axes):
    for axis in axes:
        shard = lax.psum(shard, axis)
    return shard


def taken_together(shard, axis):
    return copy_for_each(shard, axis).sum(axis=0)


def shards(design, targets, factor, weights, penalty):

    def normal_terms(rows_low):
        return summed_on_arrival(
            lax.dot_general(
                design, rows_low, (((0,), (0,)), ((), ())), preferred_element_type=jnp.float32
            ),
            ROW,
            0,
        )

    def precondition(residual):
        projected = jnp.dot(factor.T, residual, precision=lax.Precision.HIGHEST)
        projected, squares = (
            one_axis_at_a_time(projected, ROW_FEAT),
            one_axis_at_a_time(jnp.sum(residual * residual, axis=0), ROW_FEAT),
        )
        search = residual + jnp.dot(
            factor, weights[:, None] * projected, precision=lax.Precision.HIGHEST
        )
        inner = squares + jnp.sum(weights[:, None] * projected * projected, axis=0)
        return (search, inner)

    residual = normal_terms(targets)
    solution = jnp.zeros_like(residual)
    search, inner = precondition(residual)
    direction = search
    for step_index in range(ITERS):
        dir_low = direction.astype(jnp.bfloat16)
        row_values = taken_together(
            jnp.dot(design, collect(dir_low, ROW, 0), preferred_element_type=jnp.float32), FEAT
        )
        row_low = row_values.astype(jnp.bfloat16)
        dir_slice = direction
        local_part = jnp.sum(row_values * row_low.astype(jnp.float32), axis=0) / lax.axis_size(FEAT)
        local_part = local_part + penalty * jnp.sum(dir_slice * dir_slice, axis=0)
        curvature = one_axis_at_a_time(local_part, ROW_FEAT)
        hessian_dir = normal_terms(row_low) + penalty[None, :] * dir_slice
        step_size = inner / curvature
        solution = solution + step_size[None, :] * dir_slice
        residual = residual - step_size[None, :] * hessian_dir
        if step_index + 1 < ITERS:
            search, inner_next = precondition(residual)
            direction = search + (inner_next / inner)[None, :] * direction
            inner = inner_next
    return (solution, residual)


def solution(mesh):
    finer = Mesh(mesh.devices.reshape(8, 4, 4, 2), ("row_0", "row_1", "feat_0", "feat_1"))
    in_specs = (P(ROW, FEAT), P(ROW, None), P(FEAT_ROW, None), P(), P())
    out_specs = (P(FEAT_ROW, None), P(FEAT_ROW, None))
    return jax.shard_map(
        shards, mesh=finer, in_specs=in_specs, out_specs=out_specs, check_vma=False
    )
```

profile of v0, /device:TPU:1, one launch (start us, length us, event | category | flops | bytes accessed | tf_op | source)
XLA Modules:
  0.0 600.1 jit_solution(5762411116982464792)
XLA Ops:
  0.6 1.6 copy-done
  2.2 1.1 fusion.24
  3.6 50.7 %all_to_all.50 = f32[32,256,48]{1,2,0:T(8,128)} all-to-all(f32[32,256,48]{1,2,0:T(8,128)S(1)} %bitcast.76), channel_id=1, replica_groups=mesh['row_0'=8,'row_1'=4,'feat_0'=4,'feat_1'=2] {'row_0','row_1'}, dimensions={0} | all-to-all | bytes 3145728 | tf_op jit(solution)/shard_map/all_to_all | solution.py:22
  54.2 1.5 reduce_sum.171
  56.0 20.8 %psum.256 = f32[256,48]{0,1:T(8,128)S(1)} all-reduce(f32[256,48]{0,1:T(8,128)S(1)} %convolution_bitcast_fusion.5), channel_id=1, replica_groups=mesh['row_0'=8,'row_1'=4,'feat_0'=4,'feat_1'=2] {'row_0'}, use_global_device_ids=true, to_apply=%region_6.0 | all-reduce | flops 12288 | bytes 98304 | tf_op jit(solution)/shard_map/psum | solution.py:45
  76.9 13.6 %psum.257 = f32[256,48]{0,1:T(8,128)S(1)} all-reduce(f32[256,48]{0,1:T(8,128)S(1)} %psum.256), channel_id=1, replica_groups=mesh['row_0'=8,'row_1'=4,'feat_0'=4,'feat_1'=2] {'row_1'}, use_global_device_ids=true, to_apply=%region_7.0 | all-reduce | flops 12288 | bytes 98304 | tf_op jit(solution)/shard_map/psum | solution.py:45
  90.5 13.6 %psum.258 = f32[256,48]{0,1:T(8,128)S(1)} all-reduce(f32[256,48]{0,1:T(8,128)S(1)} %psum.257), channel_id=1, replica_groups=mesh['row_0'=8,'row_1'=4,'feat_0'=4,'feat_1'=2] {'feat_0'}, use_global_device_ids=true, to_apply=%region_8.0 | all-reduce | flops 12288 | bytes 98304 | tf_op jit(solution)/shard_map/psum | solution.py:45
  104.1 19.9 %psum.259 = f32[256,48]{0,1:T(8,128)S(1)} all-reduce(f32[256,48]{0,1:T(8,128)S(1)} %psum.258), channel_id=1, replica_groups=mesh['row_0'=8,'row_1'=4,'feat_0'=4,'feat_1'=2] {'feat_1'}, use_global_device_ids=true, to_apply=%region_9.0 | all-reduce | flops 12288 | bytes 98304 | tf_op jit(solution)/shard_map/psum | solution.py:45
  124.5 26.4 %all_to_all.51 = bf16[32,256,48]{1,2,0:T(8,128)(2,1)S(1)} all-to-all(bf16[32,256,48]{1,2,0:T(8,128)(2,1)S(1)} %broadcast_in_dim.12), channel_id=1, replica_groups=mesh['row_0'=8,'row_1'=4,'feat_0'=4,'feat_1'=2] {'row_0','row_1'}, dimensions={0} | all-to-all | bytes 1572864 | tf_op jit(solution)/shard_map/all_to_all | solution.py:34
  150.9 0.8 convolution_bitcast_fusion.8
  151.8 10.5 %all_to_all.52 = f32[8,128,48]{1,2,0:T(8,128)S(1)} all-to-all(f32[8,128,48]{1,2,0:T(8,128)S(1)} %broadcast_in_dim.13), channel_id=1, replica_groups=mesh['row_0'=8,'row_1'=4,'feat_0'=4,'feat_1'=2] {'feat_0','feat_1'}, dimensions={0} | all-to-all | bytes 393216 | tf_op jit(solution)/shard_map/all_to_all | solution.py:34
  162.7 1.4 copy.44
  164.1 5.2 all-to-all-start.3
  169.6 41.7 %all-reduce.2 = (f32[48]{0:T(128)S(1)}, f32[48]{0:T(128)S(1)}) all-reduce(f32[48]{0:T(128)S(1)} %multiply_reduce_fusion.5, f32[48]{0:T(128)S(1)} %multiply_add_fusion.3), channel_id=1, replica_groups=mesh['row_0'=8,'row_1'=4,'feat_0'=4,'feat_1'=2] {'row_0'}, use_global_device_ids=true, to_apply=%region_2.0 | all-reduce | flops 96 | bytes 768 | tf_op jit(solution)/shard_map/psum | solution.py:45
  211.3 9.2 %all-reduce.8 = (f32[48]{0:T(128)S(1)}, f32[48]{0:T(128)S(1)}) all-reduce(f32[48]{0:T(128)S(1)} %get-tuple-element.6, f32[48]{0:T(128)S(1)} %get-tuple-element.7), channel_id=1, replica_groups=mesh['row_0'=8,'row_1'=4,'feat_0'=4,'feat_1'=2] {'row_1'}, use_global_device_ids=true, to_apply=%region_3.0 | all-reduce | flops 96 | bytes 768 | tf_op jit(solution)/shard_map/psum | solution.py:45
  220.5 6.9 %all-reduce.5 = (f32[48]{0:T(128)S(1)}, f32[48]{0:T(128)S(1)}) all-reduce(f32[48]{0:T(128)S(1)} %get-tuple-element.18, f32[48]{0:T(128)S(1)} %get-tuple-element.19), channel_id=1, replica_groups=mesh['row_0'=8,'row_1'=4,'feat_0'=4,'feat_1'=2] {'feat_0'}, use_global_device_ids=true, to_apply=%region_4.0 | all-reduce | flops 96 | bytes 768 | tf_op jit(solution)/shard_map/psum | solution.py:45
  227.4 10.3 %all-reduce.11 = (f32[48]{0:T(128)S(1)}, f32[48]{0:T(128)S(1)}) all-reduce(f32[48]{0:T(128)S(1)} %get-tuple-element.12, f32[48]{0:T(128)S(1)} %get-tuple-element.13), channel_id=1, replica_groups=mesh['row_0'=8,'row_1'=4,'feat_0'=4,'feat_1'=2] {'feat_1'}, use_global_device_ids=true, to_apply=%region_5.0 | all-reduce | flops 96 | bytes 768 | tf_op jit(solution)/shard_map/psum | solution.py:45
  237.7 1.5 reduce_sum.177
  239.7 20.9 %all-reduce.1 = (f32[256,48]{0,1:T(8,128)S(1)}, f32[48]{0:T(128)S(1)}) all-reduce(f32[256,48]{0,1:T(8,128)S(1)} %convolution_bitcast_fusion.3, f32[48]{0:T(128)S(1)} %get-tuple-element.32), channel_id=1, replica_groups=mesh['row_0'=8,'row_1'=4,'feat_0'=4,'feat_1'=2] {'row_0'}, use_global_device_ids=true, to_apply=%region_24.0 | all-reduce | flops 12336 | bytes 98688 | tf_op jit(solution)/shard_map/psum | solution.py:45
  260.6 11.3 %all-reduce.7 = (f32[256,48]{0,1:T(8,128)S(1)}, f32[48]{0:T(128)S(1)}) all-reduce(f32[256,48]{0,1:T(8,128)S(1)} %get-tuple-element.4, f32[48]{0:T(128)S(1)} %get-tuple-element.5), channel_id=1, replica_groups=mesh['row_0'=8,'row_1'=4,'feat_0'=4,'feat_1'=2] {'row_1'}, use_global_device_ids=true, to_apply=%region_25.0 | all-reduce | flops 12336 | bytes 98688 | tf_op jit(solution)/shard_map/psum | solution.py:45
  272.0 12.1 %all-reduce.4 = (f32[256,48]{0,1:T(8,128)S(1)}, f32[48]{0:T(128)S(1)}) all-reduce(f32[256,48]{0,1:T(8,128)S(1)} %get-tuple-element.16, f32[48]{0:T(128)S(1)} %get-tuple-element.17), channel_id=1, replica_groups=mesh['row_0'=8,'row_1'=4,'feat_0'=4,'feat_1'=2] {'feat_0'}, use_global_device_ids=true, to_apply=%region_26.0 | all-reduce | flops 12336 | bytes 98688 | tf_op jit(solution)/shard_map/psum | solution.py:45
  284.0 17.8 %all-reduce.10 = (f32[256,48]{0,1:T(8,128)S(1)}, f32[48]{0:T(128)S(1)}) all-reduce(f32[256,48]{0,1:T(8,128)S(1)} %get-tuple-element.10, f32[48]{0:T(128)S(1)} %get-tuple-element.11), channel_id=1, replica_groups=mesh['row_0'=8,'row_1'=4,'feat_0'=4,'feat_1'=2] {'feat_1'}, use_global_device_ids=true, to_apply=%region_27.0 | all-reduce | flops 12336 | bytes 98688 | tf_op jit(solution)/shard_map/psum | solution.py:45
  302.0 0.5 multiply_reduce_fusion.2
  302.5 28.4 %all_to_all.53 = bf16[32,256,48]{1,2,0:T(8,128)(2,1)S(1)} all-to-all(bf16[32,256,48]{1,2,0:T(8,128)(2,1)S(1)} %broadcast_in_dim.14), channel_id=1, replica_groups=mesh['row_0'=8,'row_1'=4,'feat_0'=4,'feat_1'=2] {'row_0','row_1'}, dimensions={0} | all-to-all | bytes 1572864 | tf_op jit(solution)/shard_map/all_to_all | solution.py:34
  331.0 0.8 convolution_bitcast_fusion.7
  331.8 10.6 %all_to_all.54 = f32[8,128,48]{1,2,0:T(8,128)S(1)} all-to-all(f32[8,128,48]{1,2,0:T(8,128)S(1)} %broadcast_in_dim.15), channel_id=1, replica_groups=mesh['row_0'=8,'row_1'=4,'feat_0'=4,'feat_1'=2] {'feat_0','feat_1'}, dimensions={0} | all-to-all | bytes 393216 | tf_op jit(solution)/shard_map/all_to_all | solution.py:34
  342.8 1.4 copy.43
  344.2 5.0 all-to-all-start.6
  349.4 41.9 %psum.272 = f32[48]{0:T(128)S(1)} all-reduce(f32[48]{0:T(128)S(1)} %multiply_add_fusion.2), channel_id=1, replica_groups=mesh['row_0'=8,'row_1'=4,'feat_0'=4,'feat_1'=2] {'row_0'}, use_global_device_ids=true, to_apply=%region_32.0 | all-reduce | flops 48 | bytes 384 | tf_op jit(solution)/shard_map/psum | solution.py:45
  391.3 9.2 %psum.273 = f32[48]{0:T(128)S(1)} all-reduce(f32[48]{0:T(128)S(1)} %psum.272), channel_id=1, replica_groups=mesh['row_0'=8,'row_1'=4,'feat_0'=4,'feat_1'=2] {'row_1'}, use_global_device_ids=true, to_apply=%region_33.0 | all-reduce | flops 48 | bytes 384 | tf_op jit(solution)/shard_map/psum | solution.py:45
  400.5 6.9 %psum.274 = f32[48]{0:T(128)S(1)} all-reduce(f32[48]{0:T(128)S(1)} %psum.273), channel_id=1, replica_groups=mesh['row_0'=8,'row_1'=4,'feat_0'=4,'feat_1'=2] {'feat_0'}, use_global_device_ids=true, to_apply=%region_34.0 | all-reduce | flops 48 | bytes 384 | tf_op jit(solution)/shard_map/psum | solution.py:45
  407.3 10.3 %psum.275 = f32[48]{0:T(128)S(1)} all-reduce(f32[48]{0:T(128)S(1)} %psum.274), channel_id=1, replica_groups=mesh['row_0'=8,'row_1'=4,'feat_0'=4,'feat_1'=2] {'feat_1'}, use_global_device_ids=true, to_apply=%region_35.0 | all-reduce | flops 48 | bytes 384 | tf_op jit(solution)/shard_map/psum | solution.py:45
  417.7 1.5 reduce_sum.183
  419.6 20.9 %all-reduce = (f32[256,48]{0,1:T(8,128)S(1)}, f32[48]{0:T(128)S(1)}) all-reduce(f32[256,48]{0,1:T(8,128)S(1)} %convolution_bitcast_fusion.1, f32[48]{0:T(128)S(1)} %get-tuple-element.28), channel_id=1, replica_groups=mesh['row_0'=8,'row_1'=4,'feat_0'=4,'feat_1'=2] {'row_0'}, use_global_device_ids=true, to_apply=%region_42.0 | all-reduce | flops 12336 | bytes 98688 | tf_op jit(solution)/shard_map/psum | solution.py:45
  440.6 11.3 %all-reduce.6 = (f32[256,48]{0,1:T(8,128)S(1)}, f32[48]{0:T(128)S(1)}) all-reduce(f32[256,48]{0,1:T(8,128)S(1)} %get-tuple-element.2, f32[48]{0:T(128)S(1)} %get-tuple-element.3), channel_id=1, replica_groups=mesh['row_0'=8,'row_1'=4,'feat_0'=4,'feat_1'=2] {'row_1'}, use_global_device_ids=true, to_apply=%region_43.0 | all-reduce | flops 12336 | bytes 98688 | tf_op jit(solution)/shard_map/psum | solution.py:45
  451.9 12.1 %all-reduce.3 = (f32[256,48]{0,1:T(8,128)S(1)}, f32[48]{0:T(128)S(1)}) all-reduce(f32[256,48]{0,1:T(8,128)S(1)} %get-tuple-element.14, f32[48]{0:T(128)S(1)} %get-tuple-element.15), channel_id=1, replica_groups=mesh['row_0'=8,'row_1'=4,'feat_0'=4,'feat_1'=2] {'feat_0'}, use_global_device_ids=true, to_apply=%region_44.0 | all-reduce | flops 12336 | bytes 98688 | tf_op jit(solution)/shard_map/psum | solution.py:45
  464.0 17.8 %all-reduce.9 = (f32[256,48]{0,1:T(8,128)S(1)}, f32[48]{0:T(128)S(1)}) all-reduce(f32[256,48]{0,1:T(8,128)S(1)} %get-tuple-element.8, f32[48]{0:T(128)S(1)} %get-tuple-element.9), channel_id=1, replica_groups=mesh['row_0'=8,'row_1'=4,'feat_0'=4,'feat_1'=2] {'feat_1'}, use_global_device_ids=true, to_apply=%region_45.0 | all-reduce | flops 12336 | bytes 98688 | tf_op jit(solution)/shard_map/psum | solution.py:45
  482.4 28.6 %all_to_all.55 = bf16[32,256,48]{1,2,0:T(8,128)(2,1)S(1)} all-to-all(bf16[32,256,48]{1,2,0:T(8,128)(2,1)S(1)} %broadcast_in_dim.16), channel_id=1, replica_groups=mesh['row_0'=8,'row_1'=4,'feat_0'=4,'feat_1'=2] {'row_0','row_1'}, dimensions={0} | all-to-all | bytes 1572864 | tf_op jit(solution)/shard_map/all_to_all | solution.py:34
  511.1 0.8 convolution_bitcast_fusion.6
  512.0 10.6 %all_to_all.56 = f32[8,128,48]{1,2,0:T(8,128)S(1)} all-to-all(f32[8,128,48]{1,2,0:T(8,128)S(1)} %broadcast_in_dim.17), channel_id=1, replica_groups=mesh['row_0'=8,'row_1'=4,'feat_0'=4,'feat_1'=2] {'feat_0','feat_1'}, dimensions={0} | all-to-all | bytes 393216 | tf_op jit(solution)/shard_map/all_to_all | solution.py:34
  523.0 1.4 copy.42
  524.3 5.0 all-to-all-start.9
  529.5 42.0 %psum.284 = f32[48]{0:T(128)S(1)} all-reduce(f32[48]{0:T(128)S(1)} %multiply_add_fusion.1), channel_id=1, replica_groups=mesh['row_0'=8,'row_1'=4,'feat_0'=4,'feat_1'=2] {'row_0'}, use_global_device_ids=true, to_apply=%region_50.0 | all-reduce | flops 48 | bytes 384 | tf_op jit(solution)/shard_map/psum | solution.py:45
  571.4 9.2 %psum.285 = f32[48]{0:T(128)S(1)} all-reduce(f32[48]{0:T(128)S(1)} %psum.284), channel_id=1, replica_groups=mesh['row_0'=8,'row_1'=4,'feat_0'=4,'feat_1'=2] {'row_1'}, use_global_device_ids=true, to_apply=%region_51.0 | all-reduce | flops 48 | bytes 384 | tf_op jit(solution)/shard_map/psum | solution.py:45
  580.6 6.9 %psum.286 = f32[48]{0:T(128)S(1)} all-reduce(f32[48]{0:T(128)S(1)} %psum.285), channel_id=1, replica_groups=mesh['row_0'=8,'row_1'=4,'feat_0'=4,'feat_1'=2] {'feat_0'}, use_global_device_ids=true, to_apply=%region_52.0 | all-reduce | flops 48 | bytes 384 | tf_op jit(solution)/shard_map/psum | solution.py:45
  587.5 10.3 %psum.287 = f32[48]{0:T(128)S(1)} all-reduce(f32[48]{0:T(128)S(1)} %psum.286), channel_id=1, replica_groups=mesh['row_0'=8,'row_1'=4,'feat_0'=4,'feat_1'=2] {'feat_1'}, use_global_device_ids=true, to_apply=%region_53.0 | all-reduce | flops 48 | bytes 384 | tf_op jit(solution)/shard_map/psum | solution.py:45
  597.8 1.5 reduce_sum.189
  599.3 0.7 multiply_subtract_fusion
  (48 shorter events, 4.7 us)
Async XLA Ops:
  0.6 1.6 copy-start
  3.6 52.2 %copy-start.1 = (f32[256,256]{1,0:T(8,128)S(1)}, f32[256,256]{1,0:T(8,128)}, u32[]{:S(2)}) copy-start(f32[256,256]{1,0:T(8,128)} %param.7) | copy-start | bytes 786436
  3.6 120.4 %copy-start.2 = (f32[256]{0:T(256)S(1)}, f32[256]{0:T(256)}, u32[]{:S(2)}) copy-start(f32[256]{0:T(256)} %param.8) | copy-start | bytes 3076
  164.1 5.5 copy-start.3
  164.1 73.6 %all-to-all-start.3 = ((f32[32,256,48]{1,2,0:T(8,128)}), f32[32,256,48]{1,2,0:T(8,128)}, u32[]{:S(2)}, u32[]{:S(2)}) async-start(f32[32,256,48]{1,2,0:T(8,128)} %bitcast.73), calls=%async_computation.3 | async-start | bytes 3145728 | tf_op jit(solution)/shard_map/all_to_all | solution.py:22
  344.2 73.5 %all-to-all-start.6 = ((f32[32,256,48]{1,2,0:T(8,128)}), f32[32,256,48]{1,2,0:T(8,128)}, u32[]{:S(2)}, u32[]{:S(2)}) async-start(f32[32,256,48]{1,2,0:T(8,128)} %bitcast.75), calls=%async_computation.6 | async-start | bytes 3145728 | tf_op jit(solution)/shard_map/all_to_all | solution.py:22
  524.3 73.5 %all-to-all-start.9 = ((f32[32,256,48]{1,2,0:T(8,128)}), f32[32,256,48]{1,2,0:T(8,128)}, u32[]{:S(2)}, u32[]{:S(2)}) async-start(f32[32,256,48]{1,2,0:T(8,128)} %bitcast.74), calls=%async_computation.9 | async-start | bytes 3145728 | tf_op jit(solution)/shard_map/all_to_all | solution.py:22
where the time goes:
time: 601 us; the launch traced here: 600 us
  blocking collectives  563 us (94%)
  starting transfers between devices  15.3 us (3%)
  other arithmetic  8.02 us (1%)
  matrix products  6.96 us (1%)
  local copies, waits for them, and re-layouts  6.25 us (1%)
    psum x24, blocking collectives, one_axis_at_a_time(): shard = lax.psum(shard, axis)  397 us
    all_to_all x6, blocking collectives, copy_for_each(): lax.all_to_all(jnp.broadcast_to(shard[None], (devices, *shard.shape)), ax...  115 us
    all_to_all x1, blocking collectives, summed_on_arrival(): lax.all_to_all(pieces, axis, split_axis=0, concat_axis=0, tiled=True)  50.7 us
    all_to_all x3, starting transfers between devices, summed_on_arrival(): lax.all_to_all(pieces, axis, split_axis=0, concat_axis=0, tiled=True)  15.3 us
  transfers between devices with their start and end apart: 3, of which 0 were waited for; matrix products, arithmetic and copies ran while one was open for 0% of the time, Pallas kernels for 0%

commit v1 on v0

--- a/solution.py
+++ b/solution.py
@@ -42,7 +42,7 @@
 
 def one_axis_at_a_time(shard, axes):
     for axis in axes:
-        shard = lax.psum(shard, axis)
+        shard = jnp.sum(lax.all_gather(shard, axis), axis=0)
     return shard
 
 

time: 601 us -> 645 us (1.073)
  waiting for transfers between devices: 0.01 us -> 37.9 us
  blocking collectives: 563 us -> 540 us
  local copies, waits for them, and re-layouts: 6.25 us -> 17.9 us
  starting transfers between devices: 15.3 us -> 26.7 us
    psum x24 -> x0, blocking collectives: 397 us -> none  [one_axis_at_a_time(): shard = lax.psum(shard, axis)]
    unnamed x0 -> x20, blocking collectives: none -> 266 us
    all_gather x0 -> x12, blocking collectives: none -> 157 us  [one_axis_at_a_time(): shard = jnp.sum(lax.all_gather(shard, axis), axis=0)]
    all_to_all x1 -> x0, blocking collectives: 50.7 us -> none  [summed_on_arrival(): lax.all_to_all(pieces, axis, split_axis=0, concat_axis=0, tiled=True)]
    all_to_all x3 -> x4, waiting for transfers between devices: 0.01 us -> 37.9 us  [summed_on_arrival(): lax.all_to_all(pieces, axis, split_axis=0, concat_axis=0, tiled=True)]
    all_to_all x3 -> x4, starting transfers between devices: 15.3 us -> 26.7 us  [summed_on_arrival(): lax.all_to_all(pieces, axis, split_axis=0, concat_axis=0, tiled=True)]
    unnamed x8 -> x68, local copies, waits for them, and re-layouts: 1.61 us -> 9.3 us
  transfers between devices with their start and end apart: 3 -> 4, of which waited for: 0 -> 1; matrix products, arithmetic and copies ran while one was open for 0% -> 1% of each run, Pallas kernels for 0% -> 0%
where the time goes in v1:
time: 645 us; the launch traced here: 644 us
  blocking collectives  540 us (84%)
  waiting for transfers between devices  37.9 us (6%)
  starting transfers between devices  26.7 us (4%)
  local copies, waits for them, and re-layouts  17.9 us (3%)
  other arithmetic  10.2 us (2%)
  matrix products  6.94 us (1%)
    unnamed x20, blocking collectives  266 us
    all_gather x12, blocking collectives, one_axis_at_a_time(): shard = jnp.sum(lax.all_gather(shard, axis), axis=0)  157 us
    all_to_all x6, blocking collectives, copy_for_each(): lax.all_to_all(jnp.broadcast_to(shard[None], (devices, *shard.shape)), ax...  117 us
    all_to_all x4, waiting for transfers between devices, summed_on_arrival(): lax.all_to_all(pieces, axis, split_axis=0, concat_axis=0, tiled=True)  37.9 us
    all_to_all x4, starting transfers between devices, summed_on_arrival(): lax.all_to_all(pieces, axis, split_axis=0, concat_axis=0, tiled=True)  26.7 us
  transfers between devices with their start and end apart: 4, of which 1 were waited for; matrix products, arithmetic and copies ran while one was open for 1% of the time, Pallas kernels for 0%

profile of v1, /device:TPU:1, one launch (start us, length us, event | category | flops | bytes accessed | tf_op | source)
XLA Modules:
  0.0 643.6 jit_solution(8222325242656726787)
XLA Ops:
  0.6 1.6 copy-done
  4.7 12.3 %all-to-all-start = ((f32[32,256,48]{1,2,0:T(8,128)}), f32[32,256,48]{1,2,0:T(8,128)}, u32[]{:S(2)}, u32[]{:S(2)}) async-start(f32[32,256,48]{1,2,0:T(8,128)} %bitcast.113), calls=%async_computation | async-start | bytes 3145728 | tf_op jit(solution)/shard_map/all_to_all | solution.py:22
  17.0 37.9 %all-to-all-done = f32[32,256,48]{1,2,0:T(8,128)} async-done(((f32[32,256,48]{1,2,0:T(8,128)}), f32[32,256,48]{1,2,0:T(8,128)}, u32[]{:S(2)}, u32[]{:S(2)}) %all-to-all-start) | async-done | bytes 1572896 | tf_op jit(solution)/shard_map/all_to_all | solution.py:22
  54.8 1.5 reduce_sum.495
  56.6 19.0 %all-gather.4 = f32[2048,48]{0,1:T(8,128)S(1)} all-gather(f32[256,48]{0,1:T(8,128)S(1)} %convolution_bitcast_fusion.5), channel_id=6, replica_groups=mesh['row_0'=8,'row_1'=4,'feat_0'=4,'feat_1'=2] {'row_0'}, dimensions={0}, use_global_device_ids=true | all-gather | bytes 442368 | tf_op jit(solution)/shard_map/all_gather | solution.py:45
  75.8 10.8 %all-gather.5 = f32[1024,48]{0,1:T(8,128)S(1)} all-gather(f32[256,48]{0,1:T(8,128)S(1)} %bitcast_reduce_fusion.2), channel_id=7, replica_groups=mesh['row_0'=8,'row_1'=4,'feat_0'=4,'feat_1'=2] {'row_1'}, dimensions={0}, use_global_device_ids=true | all-gather | bytes 245760 | tf_op jit(solution)/shard_map/all_gather | solution.py:45
  86.9 9.9 %all-gather.6 = f32[1024,48]{0,1:T(8,128)S(1)} all-gather(f32[256,48]{0,1:T(8,128)S(1)} %reduce_sum.502), channel_id=8, replica_groups=mesh['row_0'=8,'row_1'=4,'feat_0'=4,'feat_1'=2] {'feat_0'}, dimensions={0}, use_global_device_ids=true | all-gather | bytes 245760 | tf_op jit(solution)/shard_map/all_gather | solution.py:45
  97.0 14.6 %all-gather.7 = f32[512,48]{0,1:T(8,128)S(1)} all-gather(f32[256,48]{0,1:T(8,128)S(1)} %reduce_sum.503), channel_id=9, replica_groups=mesh['row_0'=8,'row_1'=4,'feat_0'=4,'feat_1'=2] {'feat_1'}, dimensions={0}, use_global_device_ids=true | all-gather | bytes 147456 | tf_op jit(solution)/shard_map/all_gather | solution.py:45
  112.4 26.0 %all_to_all.50 = bf16[32,256,48]{1,2,0:T(8,128)(2,1)S(1)} all-to-all(bf16[32,256,48]{1,2,0:T(8,128)(2,1)S(1)} %broadcast_in_dim.12), channel_id=1, replica_groups=mesh['row_0'=8,'row_1'=4,'feat_0'=4,'feat_1'=2] {'row_0','row_1'}, dimensions={0} | all-to-all | bytes 1572864 | tf_op jit(solution)/shard_map/all_to_all | solution.py:34
  139.3 12.0 %all_to_all.53 = f32[8,128,48]{1,2,0:T(8,128)S(1)} all-to-all(f32[8,128,48]{1,2,0:T(8,128)S(1)} %broadcast_in_dim.13), channel_id=1, replica_groups=mesh['row_0'=8,'row_1'=4,'feat_0'=4,'feat_1'=2] {'feat_0','feat_1'}, dimensions={0} | all-to-all | bytes 393216 | tf_op jit(solution)/shard_map/all_to_all | solution.py:34
  153.2 4.9 all-to-all-start.3
  163.6 36.5 %all-reduce.24 = (f32[384]{0:T(512)S(1)}, f32[384]{0:T(512)S(1)}) all-reduce(f32[384]{0:T(512)S(1)} %dynamic-update-slice, f32[384]{0:T(512)S(1)} %add_dynamic-update-slice_fusion.2), channel_id=2, replica_groups=mesh['row_0'=8,'row_1'=4,'feat_0'=4,'feat_1'=2] {'row_0'}, use_global_device_ids=true, to_apply=%add | all-reduce | flops 768 | bytes 6144
  200.8 9.2 %all-reduce.26 = (f32[192]{0:T(256)S(1)}, f32[192]{0:T(256)S(1)}) all-reduce(f32[192]{0:T(256)S(1)} %dynamic-update-slice.1, f32[192]{0:T(256)S(1)} %dynamic-update-slice.5), channel_id=3, replica_groups=mesh['row_0'=8,'row_1'=4,'feat_0'=4,'feat_1'=2] {'row_1'}, use_global_device_ids=true, to_apply=%add.1 | all-reduce | flops 384 | bytes 3072
  210.6 7.0 %all-reduce.25 = (f32[192]{0:T(256)S(1)}, f32[192]{0:T(256)S(1)}) all-reduce(f32[192]{0:T(256)S(1)} %dynamic-update-slice.2, f32[192]{0:T(256)S(1)} %dynamic-update-slice.6), channel_id=4, replica_groups=mesh['row_0'=8,'row_1'=4,'feat_0'=4,'feat_1'=2] {'feat_0'}, use_global_device_ids=true, to_apply=%add.2 | all-reduce | flops 384 | bytes 3072
  218.3 10.1 %all-reduce.27 = (f32[96]{0:T(128)S(1)}, f32[96]{0:T(128)S(1)}) all-reduce(f32[96]{0:T(128)S(1)} %dynamic-update-slice.3, f32[96]{0:T(128)S(1)} %dynamic-update-slice.7), channel_id=5, replica_groups=mesh['row_0'=8,'row_1'=4,'feat_0'=4,'feat_1'=2] {'feat_1'}, use_global_device_ids=true, to_apply=%add.3 | all-reduce | flops 192 | bytes 1536
  228.7 1.5 reduce_sum.513
  230.6 19.2 %all-gather.16 = f32[2048,48]{0,1:T(8,128)S(1)} all-gather(f32[256,48]{0,1:T(8,128)S(1)} %convolution_bitcast_fusion.3), channel_id=18, replica_groups=mesh['row_0'=8,'row_1'=4,'feat_0'=4,'feat_1'=2] {'row_0'}, dimensions={0}, use_global_device_ids=true | all-gather | bytes 442368 | tf_op jit(solution)/shard_map/all_gather | solution.py:45
  250.1 9.2 %all-gather.17 = f32[1024,48]{0,1:T(8,128)S(1)} all-gather(f32[256,48]{0,1:T(8,128)S(1)} %bitcast_reduce_fusion.1), channel_id=19, replica_groups=mesh['row_0'=8,'row_1'=4,'feat_0'=4,'feat_1'=2] {'row_1'}, dimensions={0}, use_global_device_ids=true | all-gather | bytes 245760 | tf_op jit(solution)/shard_map/all_gather | solution.py:45
  259.6 9.2 %all-gather.18 = f32[1024,48]{0,1:T(8,128)S(1)} all-gather(f32[256,48]{0,1:T(8,128)S(1)} %reduce_sum.520), channel_id=20, replica_groups=mesh['row_0'=8,'row_1'=4,'feat_0'=4,'feat_1'=2] {'feat_0'}, dimensions={0}, use_global_device_ids=true | all-gather | bytes 245760 | tf_op jit(solution)/shard_map/all_gather | solution.py:45
  269.0 13.5 %all-gather.19 = f32[512,48]{0,1:T(8,128)S(1)} all-gather(f32[256,48]{0,1:T(8,128)S(1)} %reduce_sum.521), channel_id=21, replica_groups=mesh['row_0'=8,'row_1'=4,'feat_0'=4,'feat_1'=2] {'feat_1'}, dimensions={0}, use_global_device_ids=true | all-gather | bytes 147456 | tf_op jit(solution)/shard_map/all_gather | solution.py:45
  283.1 11.1 %all-reduce.8 = f32[384]{0:T(512)S(1)} all-reduce(f32[384]{0:T(512)S(1)} %dynamic-update-slice.8), channel_id=14, replica_groups=mesh['row_0'=8,'row_1'=4,'feat_0'=4,'feat_1'=2] {'row_0'}, use_global_device_ids=true, to_apply=%add.8 | all-reduce | flops 384 | bytes 3072
  294.5 6.0 all-reduce.9
  300.8 6.7 %all-reduce.10 = f32[192]{0:T(256)S(1)} all-reduce(f32[192]{0:T(256)S(1)} %dynamic-update-slice.10), channel_id=16, replica_groups=mesh['row_0'=8,'row_1'=4,'feat_0'=4,'feat_1'=2] {'feat_0'}, use_global_device_ids=true, to_apply=%add.10 | all-reduce | flops 192 | bytes 1536
  307.9 9.8 %all-reduce.11 = f32[96]{0:T(128)S(1)} all-reduce(f32[96]{0:T(128)S(1)} %dynamic-update-slice.11), channel_id=17, replica_groups=mesh['row_0'=8,'row_1'=4,'feat_0'=4,'feat_1'=2] {'feat_1'}, use_global_device_ids=true, to_apply=%add.11 | all-reduce | flops 96 | bytes 768
  318.3 28.8 %all_to_all.51 = bf16[32,256,48]{1,2,0:T(8,128)(2,1)S(1)} all-to-all(bf16[32,256,48]{1,2,0:T(8,128)(2,1)S(1)} %broadcast_in_dim.14), channel_id=1, replica_groups=mesh['row_0'=8,'row_1'=4,'feat_0'=4,'feat_1'=2] {'row_0','row_1'}, dimensions={0} | all-to-all | bytes 1572864 | tf_op jit(solution)/shard_map/all_to_all | solution.py:34
  348.0 10.9 %all_to_all.54 = f32[8,128,48]{1,2,0:T(8,128)S(1)} all-to-all(f32[8,128,48]{1,2,0:T(8,128)S(1)} %broadcast_in_dim.15), channel_id=1, replica_groups=mesh['row_0'=8,'row_1'=4,'feat_0'=4,'feat_1'=2] {'feat_0','feat_1'}, dimensions={0} | all-to-all | bytes 393216 | tf_op jit(solution)/shard_map/all_to_all | solution.py:34
  360.7 4.8 all-to-all-start.6
  365.7 41.8 %all-reduce.12 = f32[384]{0:T(512)S(1)} all-reduce(f32[384]{0:T(512)S(1)} %add_dynamic-update-slice_fusion.1), channel_id=22, replica_groups=mesh['row_0'=8,'row_1'=4,'feat_0'=4,'feat_1'=2] {'row_0'}, use_global_device_ids=true, to_apply=%add.12 | all-reduce | flops 384 | bytes 3072
  407.9 9.2 %all-reduce.13 = f32[192]{0:T(256)S(1)} all-reduce(f32[192]{0:T(256)S(1)} %dynamic-update-slice.13), channel_id=23, replica_groups=mesh['row_0'=8,'row_1'=4,'feat_0'=4,'feat_1'=2] {'row_1'}, use_global_device_ids=true, to_apply=%add.13 | all-reduce | flops 192 | bytes 1536
  417.5 6.8 %all-reduce.14 = f32[192]{0:T(256)S(1)} all-reduce(f32[192]{0:T(256)S(1)} %dynamic-update-slice.14), channel_id=24, replica_groups=mesh['row_0'=8,'row_1'=4,'feat_0'=4,'feat_1'=2] {'feat_0'}, use_global_device_ids=true, to_apply=%add.14 | all-reduce | flops 192 | bytes 1536
  424.6 10.3 %all-reduce.15 = f32[96]{0:T(128)S(1)} all-reduce(f32[96]{0:T(128)S(1)} %dynamic-update-slice.15), channel_id=25, replica_groups=mesh['row_0'=8,'row_1'=4,'feat_0'=4,'feat_1'=2] {'feat_1'}, use_global_device_ids=true, to_apply=%add.15 | all-reduce | flops 96 | bytes 768
  435.1 1.5 reduce_sum.531
  437.0 19.2 %all-gather.28 = f32[2048,48]{0,1:T(8,128)S(1)} all-gather(f32[256,48]{0,1:T(8,128)S(1)} %convolution_bitcast_fusion.1), channel_id=30, replica_groups=mesh['row_0'=8,'row_1'=4,'feat_0'=4,'feat_1'=2] {'row_0'}, dimensions={0}, use_global_device_ids=true | all-gather | bytes 442368 | tf_op jit(solution)/shard_map/all_gather | solution.py:45
  456.5 9.2 %all-gather.29 = f32[1024,48]{0,1:T(8,128)S(1)} all-gather(f32[256,48]{0,1:T(8,128)S(1)} %bitcast_reduce_fusion), channel_id=31, replica_groups=mesh['row_0'=8,'row_1'=4,'feat_0'=4,'feat_1'=2] {'row_1'}, dimensions={0}, use_global_device_ids=true | all-gather | bytes 245760 | tf_op jit(solution)/shard_map/all_gather | solution.py:45
  466.0 9.2 %all-gather.30 = f32[1024,48]{0,1:T(8,128)S(1)} all-gather(f32[256,48]{0,1:T(8,128)S(1)} %reduce_sum.538), channel_id=32, replica_groups=mesh['row_0'=8,'row_1'=4,'feat_0'=4,'feat_1'=2] {'feat_0'}, dimensions={0}, use_global_device_ids=true | all-gather | bytes 245760 | tf_op jit(solution)/shard_map/all_gather | solution.py:45
  475.4 13.5 %all-gather.31 = f32[512,48]{0,1:T(8,128)S(1)} all-gather(f32[256,48]{0,1:T(8,128)S(1)} %reduce_sum.539), channel_id=33, replica_groups=mesh['row_0'=8,'row_1'=4,'feat_0'=4,'feat_1'=2] {'feat_1'}, dimensions={0}, use_global_device_ids=true | all-gather | bytes 147456 | tf_op jit(solution)/shard_map/all_gather | solution.py:45
  489.5 11.1 %all-reduce.16 = f32[384]{0:T(512)S(1)} all-reduce(f32[384]{0:T(512)S(1)} %dynamic-update-slice.16), channel_id=26, replica_groups=mesh['row_0'=8,'row_1'=4,'feat_0'=4,'feat_1'=2] {'row_0'}, use_global_device_ids=true, to_apply=%add.16 | all-reduce | flops 384 | bytes 3072
  500.9 6.0 all-reduce.17
  507.2 6.7 %all-reduce.18 = f32[192]{0:T(256)S(1)} all-reduce(f32[192]{0:T(256)S(1)} %dynamic-update-slice.18), channel_id=28, replica_groups=mesh['row_0'=8,'row_1'=4,'feat_0'=4,'feat_1'=2] {'feat_0'}, use_global_device_ids=true, to_apply=%add.18 | all-reduce | flops 192 | bytes 1536
  514.3 9.8 %all-reduce.19 = f32[96]{0:T(128)S(1)} all-reduce(f32[96]{0:T(128)S(1)} %dynamic-update-slice.19), channel_id=29, replica_groups=mesh['row_0'=8,'row_1'=4,'feat_0'=4,'feat_1'=2] {'feat_1'}, use_global_device_ids=true, to_apply=%add.19 | all-reduce | flops 96 | bytes 768
  524.7 28.6 %all_to_all.52 = bf16[32,256,48]{1,2,0:T(8,128)(2,1)S(1)} all-to-all(bf16[32,256,48]{1,2,0:T(8,128)(2,1)S(1)} %broadcast_in_dim.16), channel_id=1, replica_groups=mesh['row_0'=8,'row_1'=4,'feat_0'=4,'feat_1'=2] {'row_0','row_1'}, dimensions={0} | all-to-all | bytes 1572864 | tf_op jit(solution)/shard_map/all_to_all | solution.py:34
  554.2 10.9 %all_to_all.55 = f32[8,128,48]{1,2,0:T(8,128)S(1)} all-to-all(f32[8,128,48]{1,2,0:T(8,128)S(1)} %broadcast_in_dim.17), channel_id=1, replica_groups=mesh['row_0'=8,'row_1'=4,'feat_0'=4,'feat_1'=2] {'feat_0','feat_1'}, dimensions={0} | all-to-all | bytes 393216 | tf_op jit(solution)/shard_map/all_to_all | solution.py:34
  567.0 4.8 all-to-all-start.9
  572.0 41.8 %all-reduce.20 = f32[384]{0:T(512)S(1)} all-reduce(f32[384]{0:T(512)S(1)} %add_dynamic-update-slice_fusion), channel_id=34, replica_groups=mesh['row_0'=8,'row_1'=4,'feat_0'=4,'feat_1'=2] {'row_0'}, use_global_device_ids=true, to_apply=%add.20 | all-reduce | flops 384 | bytes 3072
  614.2 9.2 %all-reduce.21 = f32[192]{0:T(256)S(1)} all-reduce(f32[192]{0:T(256)S(1)} %dynamic-update-slice.21), channel_id=35, replica_groups=mesh['row_0'=8,'row_1'=4,'feat_0'=4,'feat_1'=2] {'row_1'}, use_global_device_ids=true, to_apply=%add.21 | all-reduce | flops 192 | bytes 1536
  623.7 6.8 %all-reduce.22 = f32[192]{0:T(256)S(1)} all-reduce(f32[192]{0:T(256)S(1)} %dynamic-update-slice.22), channel_id=36, replica_groups=mesh['row_0'=8,'row_1'=4,'feat_0'=4,'feat_1'=2] {'feat_0'}, use_global_device_ids=true, to_apply=%add.22 | all-reduce | flops 192 | bytes 1536
  630.9 10.3 %all-reduce.23 = f32[96]{0:T(128)S(1)} all-reduce(f32[96]{0:T(128)S(1)} %dynamic-update-slice.23), channel_id=37, replica_groups=mesh['row_0'=8,'row_1'=4,'feat_0'=4,'feat_1'=2] {'feat_1'}, use_global_device_ids=true, to_apply=%add.23 | all-reduce | flops 96 | bytes 768
  641.3 1.5 reduce_sum.549
  (186 shorter events, 27.3 us)
Async XLA Ops:
  0.6 1.6 copy-start
  4.7 51.6 %copy-start.1 = (f32[256,256]{1,0:T(8,128)S(1)}, f32[256,256]{1,0:T(8,128)}, u32[]{:S(2)}) copy-start(f32[256,256]{1,0:T(8,128)} %param.7) | copy-start | bytes 786436
  4.7 50.1 %all-to-all-start = ((f32[32,256,48]{1,2,0:T(8,128)}), f32[32,256,48]{1,2,0:T(8,128)}, u32[]{:S(2)}, u32[]{:S(2)}) async-start(f32[32,256,48]{1,2,0:T(8,128)} %bitcast.113), calls=%async_computation | async-start | bytes 3145728 | tf_op jit(solution)/shard_map/all_to_all | solution.py:22
  56.4 55.5 %copy-start.2 = (f32[256]{0:T(256)S(1)}, f32[256]{0:T(256)}, u32[]{:S(2)}) copy-start(f32[256]{0:T(256)} %param.8) | copy-start | bytes 3076
  153.1 4.9 copy-start.7
  153.1 5.5 copy-start.6
  153.2 7.4 %copy-start.5 = (u32[256]{0:T(256)S(1)}, u32[256]{0:T(256)}, u32[]{:S(2)}) copy-start(u32[256]{0:T(256)} %constant.19) | copy-start | bytes 3076
  153.2 8.5 %copy-start.4 = (u32[256]{0:T(256)S(1)}, u32[256]{0:T(256)}, u32[]{:S(2)}) copy-start(u32[256]{0:T(256)} %constant.24) | copy-start | bytes 3076
  153.2 10.4 %copy-start.3 = (f32[48]{0:T(128)S(1)}, f32[48]{0:T(128)}, u32[]{:S(2)}) copy-start(f32[48]{0:T(128)} %param.9) | copy-start | bytes 580
  153.2 75.5 %all-to-all-start.3 = ((f32[32,256,48]{1,2,0:T(8,128)}), f32[32,256,48]{1,2,0:T(8,128)}, u32[]{:S(2)}, u32[]{:S(2)}) async-start(f32[32,256,48]{1,2,0:T(8,128)} %bitcast.110), calls=%async_computation.3 | async-start | bytes 3145728 | tf_op jit(solution)/shard_map/all_to_all | solution.py:22
  360.7 74.3 %all-to-all-start.6 = ((f32[32,256,48]{1,2,0:T(8,128)}), f32[32,256,48]{1,2,0:T(8,128)}, u32[]{:S(2)}, u32[]{:S(2)}) async-start(f32[32,256,48]{1,2,0:T(8,128)} %bitcast.112), calls=%async_computation.6 | async-start | bytes 3145728 | tf_op jit(solution)/shard_map/all_to_all | solution.py:22
  567.0 74.3 %all-to-all-start.9 = ((f32[32,256,48]{1,2,0:T(8,128)}), f32[32,256,48]{1,2,0:T(8,128)}, u32[]{:S(2)}, u32[]{:S(2)}) async-start(f32[32,256,48]{1,2,0:T(8,128)} %bitcast.111), calls=%async_computation.9 | async-start | bytes 3145728 | tf_op jit(solution)/shard_map/all_to_all | solution.py:22
